TPU v7x, 32 devices: a whole 2x2x4 slice. The times are simulated.
32 devices in a mesh: groups: 2 (over y), freq: 16 (over z, x, core).
Axes of the slice: x: 2, y: 2, z: 4, core: 2. Of those that a mesh axis runs over, the one named last changes fastest.
Arguments:
- primary_one: bfloat16 [1024, 512, 512], P(('groups', 'freq')), parts along dimension 0, may hold values from -6 to 6
- primary_two: bfloat16 [1024, 512, 512], P(('groups', 'freq')), parts along dimension 0, may hold values from -6 to 6
- primary_three: bfloat16 [1024, 512, 512], P(('groups', 'freq')), parts along dimension 0, may hold values from -6 to 6
- window_start: int32 [3, 1024, 512], P(None, ('groups', 'freq')), parts along dimension 1, may hold values from 0 to 255
- window_end: int32 [3, 1024, 512], P(None, ('groups', 'freq')), parts along dimension 1, may hold values from 257 to 512
Outputs:
- predicted: bfloat16 [1024, 512, 512], P(('groups', 'freq')), parts along dimension 0
There are 2 independent parts, one for each index of `groups`. A program takes and returns all parts, laid end to end along the dimension named above; each array names one. Nothing has to cross between parts.
Inputs may be any that keep to these rules, and one draw needn't show every extreme that they name: window_start of a trace is below its window_end.
All inputs are finite; a program needn't handle non-finite values.
Results may differ from a plain program's by a relative error of at most 0.0089.
Values may be sent and summed in bfloat16 or wider, within the bound.
A program may use at most 128 MiB of HBM per device.

v0:
```python
import jax
import jax.numpy as jnp
from jax import lax
from jax.sharding import PartitionSpec as P

F_DEV = 1


def make_table(count, samples):
    waves = jnp.arange(1, count + 1, dtype=jnp.int32)[:, None]
    times = jnp.arange(samples, dtype=jnp.int32)[None, :]
    phase = waves * times % samples
    angle = 2.0 * jnp.pi / samples * phase.astype(jnp.float32)
    both = jnp.stack([jnp.cos(angle), -jnp.sin(angle)], axis=1)
    return both.reshape(2 * count, samples).astype(jnp.bfloat16)


def spectrum(traces, start, finish, table, count):
    sources, receivers, samples = traces.shape
    times = jnp.arange(samples, dtype=jnp.int32)
    inside = (times >= start[:, :, None]) & (times < finish[:, :, None])
    windowed = jnp.where(inside, traces, jnp.zeros_like(traces))
    flat = windowed.reshape(sources * receivers, samples)
    spec = lax.dot_general(
        table, flat, (((1,), (1,)), ((), ())), preferred_element_type=jnp.float32
    )
    spec = spec * (1.0 / jnp.sqrt(jnp.float32(samples)))
    return spec.astype(jnp.bfloat16).reshape(count, 2, sources, receivers)


def correlate(first, second):
    swapped = jnp.stack([first[:, 1], -first[:, 0]], axis=1)
    left = jnp.stack([first, swapped], axis=1)
    cross = jnp.einsum("fkcsr,fcur->fksu", left, second, preferred_element_type=jnp.float32)
    cross = cross * (1.0 / jnp.sqrt(jnp.float32(first.shape[3])))
    return cross.astype(jnp.bfloat16)


def convolve(cross, third):
    right = jnp.stack(
        [
            jnp.stack([third[:, 0], -third[:, 1]], axis=1),
            jnp.stack([third[:, 1], third[:, 0]], axis=1),
        ],
        axis=1,
    )
    multiple = jnp.einsum("fcsu,fkcur->fksr", cross, right, preferred_element_type=jnp.float32)
    multiple = multiple * (1.0 / jnp.sqrt(jnp.float32(third.shape[2])))
    return multiple.astype(jnp.bfloat16)


def on_device(primary_one, primary_two, primary_three, window_start, window_end):
    samples = primary_one.shape[2]
    count = F_DEV * lax.axis_size("freq")
    table = make_table(count, samples)
    spec_one = spectrum(primary_one, window_start[0], window_end[0], table, count)
    spec_two = spectrum(primary_two, window_start[1], window_end[1], table, count)
    spec_three = spectrum(primary_three, window_start[2], window_end[2], table, count)
    first, second, third = (
        lax.all_to_all(spec_one, "freq", split_axis=0, concat_axis=2, tiled=True),
        lax.all_to_all(spec_two, "freq", split_axis=0, concat_axis=2, tiled=True),
        lax.all_to_all(spec_three, "freq", split_axis=0, concat_axis=2, tiled=True),
    )
    cross = correlate(first, second)
    multiple = convolve(cross, third)
    piece = lax.all_to_all(multiple, "freq", split_axis=2, concat_axis=0, tiled=True)
    waves, parts, sources, receivers = piece.shape
    flat = piece.reshape(waves * parts, sources * receivers)
    timed = lax.dot_general(
        flat, table, (((0,), (0,)), ((), ())), preferred_element_type=jnp.float32
    )
    timed = timed * (1.0 / jnp.sqrt(jnp.float32(count)))
    return timed.astype(jnp.bfloat16).reshape(sources, receivers, samples)


def solution(mesh):
    return jax.shard_map(
        on_device,
        mesh=mesh,
        in_specs=(
            P(("groups", "freq"), None, None),
            P(("groups", "freq"), None, None),
            P(("groups", "freq"), None, None),
            P(None, ("groups", "freq"), None),
            P(None, ("groups", "freq"), None),
        ),
        out_specs=P(("groups", "freq"), None, None),
        check_vma=False,
    )
```

profile of v0, /device:TPU:1, one launch (start us, length us, event | category | flops | bytes accessed | tf_op | source)
XLA Modules:
  0.0 175.8 jit_solution(10314917544340904207)
XLA Ops:
  0.9 0.9 slice_bitcast_fusion.2
  2.1 22.8 %fusion.1 = (bf16[32,512,512]{2,1,0:T(8,128)(2,1)}, bf16[32,512,512]{2,1,0:T(8,128)(2,1)}) fusion(bf16[32,512,512]{2,1,0:T(8,128)(2,1)} %param.7, s32[32,512]{1,0:T(8,128)S(1)} %get-tuple-element.15, s32[32,512]{1,0:T(8,128)S(1)} %get-tuple-element.12, bf16[32,512,512]{2,1,0:T(8,128)(2,1)} %param.5, s32[32,512]{1,0:T(8,128)S(1)} %get-tuple-element.14, ...), kind=kLoop, calls=%fused_computation.8 | loop fusion | flops 67108864 | bytes 67371008 | tf_op jit(solution)/shard_map/jit(_where)/select_n | solution.py:22
  24.9 10.7 %fusion.6 = bf16[32,16384]{1,0:T(8,128)(2,1)S(1)} fusion(bf16[32,512]{1,0:T(8,128)(2,1)S(1)} %convert_element_type.64, bf16[16384,512]{1,0:T(8,128)(2,1)} %bitcast.108), kind=kOutput, calls=%fused_computation.16 | convolution fusion | flops 537919488 | bytes 17858560 | tf_op jit(solution)/shard_map/dot_general | solution.py:24
  35.7 1.3 copy.43
  37.0 7.3 %all-to-all-start = ((bf16[16,2,32,512]{3,2,1,0:T(8,128)(2,1)}), bf16[16,2,32,512]{3,2,1,0:T(8,128)(2,1)S(1)}, u32[]{:S(2)}, u32[]{:S(2)}) async-start(bf16[16,2,32,512]{3,2,1,0:T(8,128)(2,1)} %bitcast.47), calls=%async_computation | async-start | bytes 2097152 | tf_op jit(solution)/shard_map/all_to_all | solution.py:62
  44.3 10.7 %fusion.7 = bf16[32,16384]{1,0:T(8,128)(2,1)S(1)} fusion(bf16[32,512]{1,0:T(8,128)(2,1)S(1)} %convert_element_type.64, bf16[16384,512]{1,0:T(8,128)(2,1)} %bitcast.107), kind=kOutput, calls=%fused_computation.17 | convolution fusion | flops 537919488 | bytes 17858560 | tf_op jit(solution)/shard_map/dot_general | solution.py:24
  55.0 1.3 copy.44
  56.4 11.1 %all-to-all-done = bf16[16,2,32,512]{3,2,1,0:T(8,128)(2,1)S(1)} async-done(((bf16[16,2,32,512]{3,2,1,0:T(8,128)(2,1)}), bf16[16,2,32,512]{3,2,1,0:T(8,128)(2,1)S(1)}, u32[]{:S(2)}, u32[]{:S(2)}) %all-to-all-start) | async-done | bytes 1048608 | tf_op jit(solution)/shard_map/all_to_all | solution.py:62
  67.5 6.5 %all-to-all-start.1 = ((bf16[16,2,32,512]{3,2,1,0:T(8,128)(2,1)}), bf16[16,2,32,512]{3,2,1,0:T(8,128)(2,1)S(1)}, u32[]{:S(2)}, u32[]{:S(2)}) async-start(bf16[16,2,32,512]{3,2,1,0:T(8,128)(2,1)} %bitcast.115), calls=%async_computation.1 | async-start | bytes 2097152 | tf_op jit(solution)/shard_map/all_to_all | solution.py:60
  74.0 12.0 %fusion.5 = bf16[32,512,512]{2,1,0:T(8,128)(2,1)} fusion(bf16[32,512,512]{2,1,0:T(8,128)(2,1)} %param.6, s32[32,512]{1,0:T(8,128)S(1)} %get-tuple-element.16, s32[32,512]{1,0:T(8,128)S(1)} %get-tuple-element.13), kind=kLoop, calls=%fused_computation.12 | loop fusion | flops 33554432 | bytes 33685504 | tf_op jit(solution)/shard_map/jit(_where)/select_n | solution.py:22
  86.0 10.7 %fusion.8 = bf16[32,16384]{1,0:T(8,128)(2,1)S(1)} fusion(bf16[32,512]{1,0:T(8,128)(2,1)S(1)} %convert_element_type.64, bf16[16384,512]{1,0:T(8,128)(2,1)} %bitcast.106), kind=kOutput, calls=%fused_computation.18 | convolution fusion | flops 537919488 | bytes 17858560 | tf_op jit(solution)/shard_map/dot_general | solution.py:24
  96.7 1.3 copy.45
  98.1 1.0 copy-done
  99.0 6.0 %all-to-all-start.2 = ((bf16[16,2,32,512]{3,2,1,0:T(8,128)(2,1)}), bf16[16,2,32,512]{3,2,1,0:T(8,128)(2,1)S(1)}, u32[]{:S(2)}, u32[]{:S(2)}) async-start(bf16[16,2,32,512]{3,2,1,0:T(8,128)(2,1)} %bitcast.53), calls=%async_computation.2 | async-start | bytes 2097152 | tf_op jit(solution)/shard_map/all_to_all | solution.py:61
  105.5 1.0 copy.41
  106.6 1.3 copy.34
  107.9 1.1 maximum_bitcast_fusion.14
  109.0 2.7 %maximum_bitcast_fusion.12 = (bf16[1,1,2,512,512]{3,4,2,1,0:T(8,128)(2,1)}, bf16[1,1,2,512,512]{3,4,2,1,0:T(8,128)(2,1)}) fusion(bf16[1,1,512,512]{2,3,1,0:T(8,128)(2,1)S(1)} %neg.23, bf16[1,1,512,512]{2,3,1,0:T(8,128)(2,1)} %copy.41, bf16[1,1,512,512]{2,3,1,0:T(8,128)(2,1)S(1)} %copy.42), kind=kLoop, calls=%fused_computation.33 | loop fusion | flops 1048576 | bytes 3670016 | tf_op jit(solution)/shard_map/stack | solution.py:40
  111.7 16.5 %all-to-all-done.2 = bf16[16,2,32,512]{3,2,1,0:T(8,128)(2,1)S(1)} async-done(((bf16[16,2,32,512]{3,2,1,0:T(8,128)(2,1)}), bf16[16,2,32,512]{3,2,1,0:T(8,128)(2,1)S(1)}, u32[]{:S(2)}, u32[]{:S(2)}) %all-to-all-start.2) | async-done | bytes 1048608 | tf_op jit(solution)/shard_map/all_to_all | solution.py:61
  128.2 1.0 copy.35
  129.3 4.5 %fusion.18 = bf16[1,2,512,512]{2,3,1,0:T(8,128)(2,1)S(1)} fusion(bf16[1,1,2,512,512]{3,4,2,1,0:T(8,128)(2,1)} %get-tuple-element.10, bf16[1,1,2,512,512]{3,4,2,1,0:T(8,128)(2,1)} %get-tuple-element.9, bf16[2,512,512,1]{2,1,0,3:T(8,128)(2,1)} %bitcast.119, bf16[1,1,2,512,512]{4,3,2,1,0:T(8,128)(2,1)} %maximum_bitcast_fusion.14, ...), kind=kOutput, calls=%fused_computation.32 | convolution fusion | flops 2151677952 | bytes 6291456 | tf_op jit(solution)/shard_map/fcsu,fkcur->fksr/dot_general | solution.py:47
  133.8 1.0 copy.36
  134.8 31.5 %all_to_all.66 = bf16[1,2,512,512]{3,1,0,2:T(2,128)(2,1)S(1)} all-to-all(bf16[1,2,512,512]{3,1,0,2:T(2,128)(2,1)S(1)} %copy.36), channel_id=1, replica_groups=mesh['groups'=2,'freq'=16] {'freq'}, dimensions={2} | all-to-all | bytes 2097152 | tf_op jit(solution)/shard_map/all_to_all | solution.py:66
  167.2 8.6 %multiply_convert_fusion = bf16[16384,512]{1,0:T(8,128)(2,1)} fusion(bf16[32,16384]{1,0:T(8,128)(2,1)S(1)} %bitcast.109, bf16[32,512]{1,0:T(8,128)(2,1)S(1)} %convert_element_type.64), kind=kOutput, calls=%fused_computation | convolution fusion | flops 553648128 | bytes 17858560 | tf_op jit(solution)/shard_map/dot_general | solution.py:69
  (16 shorter events, 2.6 us)
Async XLA Ops:
  37.0 30.5 %all-to-all-start = ((bf16[16,2,32,512]{3,2,1,0:T(8,128)(2,1)}), bf16[16,2,32,512]{3,2,1,0:T(8,128)(2,1)S(1)}, u32[]{:S(2)}, u32[]{:S(2)}) async-start(bf16[16,2,32,512]{3,2,1,0:T(8,128)(2,1)} %bitcast.47), calls=%async_computation | async-start | bytes 2097152 | tf_op jit(solution)/shard_map/all_to_all | solution.py:62
  67.5 30.6 %all-to-all-start.1 = ((bf16[16,2,32,512]{3,2,1,0:T(8,128)(2,1)}), bf16[16,2,32,512]{3,2,1,0:T(8,128)(2,1)S(1)}, u32[]{:S(2)}, u32[]{:S(2)}) async-start(bf16[16,2,32,512]{3,2,1,0:T(8,128)(2,1)} %bitcast.115), calls=%async_computation.1 | async-start | bytes 2097152 | tf_op jit(solution)/shard_map/all_to_all | solution.py:60
  98.1 1.0 copy-start
  99.0 29.2 %all-to-all-start.2 = ((bf16[16,2,32,512]{3,2,1,0:T(8,128)(2,1)}), bf16[16,2,32,512]{3,2,1,0:T(8,128)(2,1)S(1)}, u32[]{:S(2)}, u32[]{:S(2)}) async-start(bf16[16,2,32,512]{3,2,1,0:T(8,128)(2,1)} %bitcast.53), calls=%async_computation.2 | async-start | bytes 2097152 | tf_op jit(solution)/shard_map/all_to_all | solution.py:61
where the time goes:
time: 176 us
  matrix products  45.3 us (26%)
  other arithmetic  39 us (22%)
  blocking collectives  31.5 us (18%)
  waiting for transfers between devices  27.6 us (16%)
  starting transfers between devices  19.8 us (11%)
  local copies, waits for them, and re-layouts  12.4 us (7%)
    select_n x2, other arithmetic, spectrum(): windowed = jnp.where(inside, traces, jnp.zeros_like(traces))  34.8 us
    dot_general x3, matrix products, spectrum(): lax.dot_general(table, flat, (((1,), (1,)), ((), ())), preferred_element_...  32.2 us
    all_to_all x1, blocking collectives, on_device(): lax.all_to_all(multiple, 'freq', split_axis=2, concat_axis=0, tiled=True)  31.5 us
    all_to_all x1, waiting for transfers between devices, on_device(): lax.all_to_all(spec_two, 'freq', split_axis=0, concat_axis=2, tiled=True)  16.5 us
    all_to_all x1, waiting for transfers between devices, on_device(): lax.all_to_all(spec_three, 'freq', split_axis=0, concat_axis=2, tiled=True)  11.1 us
    dot_general x1, matrix products, on_device(): lax.dot_general(flat, table, (((0,), (0,)), ((), ())), preferred_element_...  8.56 us
    all_to_all x1, starting transfers between devices, on_device(): lax.all_to_all(spec_three, 'freq', split_axis=0, concat_axis=2, tiled=True)  7.31 us
    unnamed x8, local copies, waits for them, and re-layouts  6.72 us
  transfers between devices with their start and end apart: 3, of which 2 were waited for; matrix products, arithmetic and copies ran while one was open for 24% of the time, Pallas kernels for 0%

commit v1 on v0

--- a/solution.py
+++ b/solution.py
@@ -1,9 +1,15 @@
+import functools
+
 import jax
 import jax.numpy as jnp
 from jax import lax
+from jax.experimental import pallas as pl
+from jax.experimental.pallas import tpu as pltpu
 from jax.sharding import PartitionSpec as P
 
 F_DEV = 1
+GROUP = 16
+LANES = 128
 
 
 def make_table(count, samples):
@@ -13,6 +19,189 @@
     angle = 2.0 * jnp.pi / samples * phase.astype(jnp.float32)
     both = jnp.stack([jnp.cos(angle), -jnp.sin(angle)], axis=1)
     return both.reshape(2 * count, samples).astype(jnp.bfloat16)
+
+
+def exchange_kernel(
+    n, sub, one_ref, two_ref, three_ref, start_ref, end_ref, table_ref, out_ref,
+    buf, scr, stage, r1, r2, r3, gw, mbuf,
+    load_sem, send_sem, r1_sem, r23_sem, out_sem,
+):
+    me = lax.axis_index("freq")
+    sources, receivers, samples = one_ref.shape
+    half = n // 2
+    side = me // half
+    quarter = n // 4
+    rows_q = quarter * sources
+    n_sub = GROUP // sub
+    total = sources // sub
+
+    def peer_far(q):
+        return (1 - side) * half + lax.rem(me + q, half)
+
+    def peer_near(q):
+        return side * half + lax.rem(me + q, half)
+
+    barrier = pltpu.get_barrier_semaphore()
+
+    @pl.loop(1, n)
+    def _(q):
+        pl.semaphore_signal(
+            barrier, inc=1, device_id={"freq": lax.rem(me + q, n)},
+            device_id_type=pl.DeviceIdType.MESH,
+        )
+
+    sets = ((two_ref, 1, r2), (three_ref, 2, r3), (one_ref, 0, r1))
+
+    def load(ref, i, slot):
+        return pltpu.make_async_copy(
+            ref.at[pl.ds(i * sub, sub)], buf.at[slot], load_sem.at[slot]
+        )
+
+    load(sets[0][0], 0, 0).start()
+    scale_t = 1.0 / (samples ** 0.5)
+
+    for k, (ref, which, landing) in enumerate(sets):
+        if k < 2:
+            arrive = r23_sem.at[k]
+        else:
+            arrive = r1_sem.at[me // quarter]
+
+        @pl.loop(0, sources // GROUP)
+        def _(g):
+            @pl.loop(0, n_sub)
+            def _(j):
+                i = g * n_sub + j
+                slot = lax.rem(i, 2)
+
+                @pl.when(i + 1 < total)
+                def _():
+                    load(ref, i + 1, 1 - slot).start()
+
+                if k < 2:
+                    @pl.when(i + 1 == total)
+                    def _():
+                        load(sets[k + 1][0], 0, 0).start()
+
+                load(ref, i, slot).wait()
+                for s in range(sub):
+                    row = i * sub + s
+                    first = start_ref[which, pl.ds(row, 1), :]
+                    last = end_ref[which, pl.ds(row, 1), :]
+                    first = jnp.broadcast_to(first, (LANES, receivers)).T
+                    last = jnp.broadcast_to(last, (LANES, receivers)).T
+                    lane = lax.broadcasted_iota(jnp.int32, (receivers, LANES), 1)
+                    pieces = []
+                    for c in range(samples // LANES):
+                        x = buf[slot, s, :, c * LANES:(c + 1) * LANES]
+                        t = lane + c * LANES
+                        keep = (t >= first) & (t < last)
+                        pieces.append(jnp.where(keep, x, jnp.zeros_like(x)))
+                    windowed = jnp.concatenate(pieces, axis=1)
+                    spec = lax.dot_general(
+                        table_ref[...], windowed, (((1,), (1,)), ((), ())),
+                        preferred_element_type=jnp.float32,
+                    )
+                    scr[j * sub + s] = spec * scale_t
+
+            at = pl.ds(pl.multiple_of(g * GROUP, GROUP), GROUP)
+            for w in range(2 * n):
+                stage[k, w // 2, w % 2, at, :] = scr[:, w, :].astype(jnp.bfloat16)
+
+            if k == 0:
+                @pl.when(g == 0)
+                def _():
+                    pl.semaphore_wait(barrier, n - 1)
+
+                send_rows(k, g * GROUP, GROUP, landing, arrive, me, n, sources,
+                          half, peer_far, peer_near, stage, send_sem)
+
+        if k > 0:
+            send_rows(k, 0, sources, landing, arrive, me, n, sources,
+                      half, peer_far, peer_near, stage, send_sem)
+
+    def drain(ref, sem):
+        pltpu.make_async_copy(ref, ref, sem).wait()
+
+    drain(r2, r23_sem.at[0])
+    drain(r3, r23_sem.at[1])
+    scale_g = 1.0 / ((n * sources) ** 0.5)
+    scale_m = 1.0 / (receivers ** 0.5)
+    width = 256
+
+    @pl.loop(0, receivers // width)
+    def _(b):
+        cols = pl.ds(pl.multiple_of(b * width, width), width)
+        ct = r2[0, :, cols].T
+        dt = r2[1, :, cols].T
+        e = r3[0]
+        f = r3[1]
+        dot = functools.partial(jnp.dot, preferred_element_type=jnp.float32)
+        gw[cols, :receivers] = ((dot(ct, e) + dot(dt, f)) * scale_g).astype(jnp.bfloat16)
+        gw[cols, receivers:] = ((dot(ct, f) - dot(dt, e)) * scale_g).astype(jnp.bfloat16)
+
+    @pl.loop(0, 4)
+    def _(step):
+        other = (1 - side) * 2 + step
+        own = side * 2 + lax.rem(step, 2)
+        z = jnp.where(step < 2, other, own)
+        rows = pl.ds(pl.multiple_of(z * rows_q, rows_q), rows_q)
+        block = r1.at[:, rows, :]
+        drain(block, r1_sem.at[z])
+        both = jnp.concatenate([r1[0, rows, :], r1[1, rows, :]], axis=0)
+        prod = jnp.dot(both, gw[...], preferred_element_type=jnp.float32)
+        re = prod[:rows_q, :receivers] - prod[rows_q:, receivers:]
+        im = prod[:rows_q, receivers:] + prod[rows_q:, :receivers]
+        mbuf[0, rows, :] = (re * scale_m).astype(jnp.bfloat16)
+        mbuf[1, rows, :] = (im * scale_m).astype(jnp.bfloat16)
+
+        @pl.loop(0, quarter)
+        def _(q):
+            p = z * quarter + lax.rem(me + q, quarter)
+            src = mbuf.at[:, pl.ds(pl.multiple_of(p * sources, sources), sources), :]
+
+            @pl.when(p != me)
+            def _():
+                pltpu.make_async_remote_copy(
+                    src_ref=src, dst_ref=out_ref.at[me],
+                    send_sem=send_sem.at[3], recv_sem=out_sem,
+                    device_id={"freq": p}, device_id_type=pl.DeviceIdType.MESH,
+                ).start()
+
+            @pl.when(p == me)
+            def _():
+                pltpu.make_async_copy(src, out_ref.at[me], out_sem).start()
+
+    drain(out_ref, out_sem)
+    for k in range(3):
+        drain(stage.at[k, pl.ds(0, n - 1)], send_sem.at[k])
+    drain(out_ref.at[pl.ds(0, n - 1)], send_sem.at[3])
+
+
+def send_rows(k, base, count, landing, arrive, me, n, sources, half,
+              peer_far, peer_near, stage, send_sem):
+    if not isinstance(base, int):
+        base = pl.multiple_of(base, GROUP)
+    here = pl.ds(base, count)
+    there = pl.ds(pl.multiple_of(me * sources + base, GROUP), count)
+
+    def send(p):
+        pltpu.make_async_remote_copy(
+            src_ref=stage.at[k, p, :, here, :], dst_ref=landing.at[:, there, :],
+            send_sem=send_sem.at[k], recv_sem=arrive,
+            device_id={"freq": p}, device_id_type=pl.DeviceIdType.MESH,
+        ).start()
+
+    @pl.loop(0, half)
+    def _(q):
+        send(peer_far(q))
+
+    @pl.loop(1, half)
+    def _(q):
+        send(peer_near(q))
+
+    pltpu.make_async_copy(
+        stage.at[k, me, :, here, :], landing.at[:, there, :], arrive
+    ).start()
 
 
 def spectrum(traces, start, finish, table, count):
@@ -49,7 +238,7 @@
     return multiple.astype(jnp.bfloat16)
 
 
-def on_device(primary_one, primary_two, primary_three, window_start, window_end):
+def plain_on_device(primary_one, primary_two, primary_three, window_start, window_end):
     samples = primary_one.shape[2]
     count = F_DEV * lax.axis_size("freq")
     table = make_table(count, samples)
@@ -66,6 +255,53 @@
     piece = lax.all_to_all(multiple, "freq", split_axis=2, concat_axis=0, tiled=True)
     waves, parts, sources, receivers = piece.shape
     flat = piece.reshape(waves * parts, sources * receivers)
+    timed = lax.dot_general(
+        flat, table, (((0,), (0,)), ((), ())), preferred_element_type=jnp.float32
+    )
+    timed = timed * (1.0 / jnp.sqrt(jnp.float32(count)))
+    return timed.astype(jnp.bfloat16).reshape(sources, receivers, samples)
+
+
+def on_device(primary_one, primary_two, primary_three, window_start, window_end):
+    sources, receivers, samples = primary_one.shape
+    n = lax.axis_size("freq")
+    if sources % GROUP or n % 4 or receivers % 256 or samples % LANES:
+        return plain_on_device(
+            primary_one, primary_two, primary_three, window_start, window_end
+        )
+    count = F_DEV * n
+    table = make_table(count, samples)
+    sub = max(1, min(GROUP // 2, (2 << 20) // (receivers * samples * 2)))
+    bf = jnp.bfloat16
+    whole = n * sources
+    vmem = pl.BlockSpec(memory_space=pltpu.VMEM)
+    hbm = pl.BlockSpec(memory_space=pl.ANY)
+    piece = pl.pallas_call(
+        functools.partial(exchange_kernel, n, sub),
+        out_shape=jax.ShapeDtypeStruct((n, 2, sources, receivers), bf),
+        in_specs=[hbm, hbm, hbm, vmem, vmem, vmem],
+        out_specs=vmem,
+        scratch_shapes=[
+            pltpu.VMEM((2, sub, receivers, samples), bf),
+            pltpu.VMEM((GROUP, 2 * count, receivers), jnp.float32),
+            pltpu.VMEM((3, n, 2, sources, receivers), bf),
+            pltpu.VMEM((2, whole, receivers), bf),
+            pltpu.VMEM((2, whole, receivers), bf),
+            pltpu.VMEM((2, whole, receivers), bf),
+            pltpu.VMEM((receivers, 2 * receivers), bf),
+            pltpu.VMEM((2, whole, receivers), bf),
+            pltpu.SemaphoreType.DMA((2,)),
+            pltpu.SemaphoreType.DMA((4,)),
+            pltpu.SemaphoreType.DMA((4,)),
+            pltpu.SemaphoreType.DMA((2,)),
+            pltpu.SemaphoreType.DMA,
+        ],
+        compiler_params=pltpu.CompilerParams(
+            collective_id=0, has_side_effects=True, vmem_limit_bytes=67000000,
+        ),
+        name="exchange",
+    )(primary_one, primary_two, primary_three, window_start, window_end, table)
+    flat = piece.reshape(2 * count, sources * receivers)
     timed = lax.dot_general(
         flat, table, (((0,), (0,)), ((), ())), preferred_element_type=jnp.float32
     )

time: 176 us -> 125 us (0.71)
  Pallas kernels: 0 us -> 113 us
  other arithmetic: 39 us -> 0.23 us
  matrix products: 45.3 us -> 8.56 us
  blocking collectives: 31.5 us -> 0 us
  waiting for transfers between devices: 27.6 us -> 0 us
  starting transfers between devices: 19.8 us -> 0 us
  local copies, waits for them, and re-layouts: 12.4 us -> 2.48 us
    pallas_call x0 -> x1, Pallas kernels: none -> 113 us  [on_device(): pl.pallas_call(functools.partial(exchange_kernel, n, sub), out_shape=jax....]
    dot_general x4 -> x0, matrix products: 36.7 us -> none  [the longest x3 32.2 us: spectrum(): lax.dot_general(table, flat, (((1,), (1,)), ((), ())), preferred_element_...]
    select_n x2 -> x0, other arithmetic: 34.8 us -> none  [spectrum(): windowed = jnp.where(inside, traces, jnp.zeros_like(traces))]
    all_to_all x1 -> x0, blocking collectives: 31.5 us -> none  [on_device(): lax.all_to_all(multiple, 'freq', split_axis=2, concat_axis=0, tiled=True)]
    all_to_all x3 -> x0, waiting for transfers between devices: 27.6 us -> none  [the longest x1 16.5 us: on_device(): lax.all_to_all(spec_two, 'freq', split_axis=0, concat_axis=2, tiled=True)]
    all_to_all x3 -> x0, starting transfers between devices: 19.8 us -> none  [the longest x1 7.31 us: on_device(): lax.all_to_all(spec_three, 'freq', split_axis=0, concat_axis=2, tiled=True)]
    unnamed x8 -> x3, local copies, waits for them, and re-layouts: 6.72 us -> 1.81 us
    another operation x4 -> x0, other arithmetic: 4.02 us -> none  [the longest x1 2.74 us: convolve(): jnp.stack([jnp.stack([third[:, 0], -third[:, 1]], axis=1), jnp.stack([thi...]
  transfers between devices with their start and end apart: 3 -> 0, of which waited for: 2 -> 0; matrix products, arithmetic and copies ran while one was open for 24% -> 0% of each run, Pallas kernels for 0% -> 0%
where the time goes in v1:
time: 125 us; the launch traced here: 124 us
  Pallas kernels  113 us (90%)
  matrix products  8.56 us (7%)
  local copies, waits for them, and re-layouts  2.48 us (2%)
    pallas_call x1, Pallas kernels, on_device(): pl.pallas_call(functools.partial(exchange_kernel, n, sub), out_shape=jax....  113 us
    dot_general x1, matrix products, on_device(): lax.dot_general(flat, table, (((0,), (0,)), ((), ())), preferred_element_...  8.56 us

profile of v1, /device:TPU:1, one launch (start us, length us, event | category | flops | bytes accessed | tf_op | source)
XLA Modules:
  0.0 123.8 jit_solution(12458524266352485743)
XLA Ops:
  0.0 0.2 fusion.6
  0.3 0.6 convert_element_type.26.table_ref
  0.9 0.0 copy-start
  0.9 112.5 %exchange.1 = bf16[16,2,32,512]{3,2,1,0:T(8,128)(2,1)} custom-call(bf16[32,512,512]{2,1,0:T(8,128)(2,1)} %one_ref.1, bf16[32,512,512]{2,1,0:T(8,128)(2,1)} %two_ref.1, bf16[32,512,512]{2,1,0:T(8,128)(2,1)} %three_ref.1, s32[3,32,512]{2,1,0:T(8,128)} %start_ref.1, s32[3,32,512]{2,1,0:T(8,128)} %end_ref.1, bf16[32,512]{1,0:T(8,128)(2,1)} %convert_element_type.26.table_ref), custom_call_target="tpu_custom_call" | custom-call | tf_op jit(solution)/shard_map/exchange/pallas_call | solution.py:279
  113.5 1.8 %copy.7 = bf16[4,8,32,512]{3,1,2,0:T(8,128)(2,1)S(1)} copy(bf16[4,8,32,512]{3,2,1,0:T(8,128)(2,1)} %bitcast.7) | data formatting | bytes 2097152
  115.3 0.0 copy-done
  115.3 8.6 %multiply_convert_fusion = bf16[16384,512]{1,0:T(8,128)(2,1)} fusion(bf16[32,16384]{1,0:T(8,128)(2,1)S(1)} %bitcast.6, bf16[32,512]{1,0:T(8,128)(2,1)S(1)} %copy-done), kind=kOutput, calls=%fused_computation | convolution fusion | flops 553648128 | bytes 17858560 | tf_op jit(solution)/shard_map/dot_general | solution.py:305
  (3 shorter events, 0.0 us)
Async XLA Ops:
  0.9 114.4 %copy-start = (bf16[32,512]{1,0:T(8,128)(2,1)S(1)}, bf16[32,512]{1,0:T(8,128)(2,1)}, u32[]{:S(2)}) copy-start(bf16[32,512]{1,0:T(8,128)(2,1)} %convert_element_type.26.table_ref) | copy-start | bytes 98308

commit v2 on v1

--- a/solution.py
+++ b/solution.py
@@ -30,8 +30,6 @@
     sources, receivers, samples = one_ref.shape
     half = n // 2
     side = me // half
-    quarter = n // 4
-    rows_q = quarter * sources
     n_sub = GROUP // sub
     total = sources // sub
 
@@ -64,7 +62,7 @@
         if k < 2:
             arrive = r23_sem.at[k]
         else:
-            arrive = r1_sem.at[me // quarter]
+            arrive = r1_sem.at[me]
 
         @pl.loop(0, sources // GROUP)
         def _(g):
@@ -85,10 +83,13 @@
                 load(ref, i, slot).wait()
                 for s in range(sub):
                     row = i * sub + s
-                    first = start_ref[which, pl.ds(row, 1), :]
-                    last = end_ref[which, pl.ds(row, 1), :]
-                    first = jnp.broadcast_to(first, (LANES, receivers)).T
-                    last = jnp.broadcast_to(last, (LANES, receivers)).T
+                    packed = (
+                        start_ref[which, pl.ds(row, 1), :] * 4096
+                        + end_ref[which, pl.ds(row, 1), :]
+                    )
+                    packed = jnp.broadcast_to(packed, (LANES, receivers)).T
+                    first = packed >> 12
+                    last = packed & 4095
                     lane = lax.broadcasted_iota(jnp.int32, (receivers, LANES), 1)
                     pieces = []
                     for c in range(samples // LANES):
@@ -139,37 +140,31 @@
         gw[cols, :receivers] = ((dot(ct, e) + dot(dt, f)) * scale_g).astype(jnp.bfloat16)
         gw[cols, receivers:] = ((dot(ct, f) - dot(dt, e)) * scale_g).astype(jnp.bfloat16)
 
-    @pl.loop(0, 4)
+    @pl.loop(0, n)
     def _(step):
-        other = (1 - side) * 2 + step
-        own = side * 2 + lax.rem(step, 2)
-        z = jnp.where(step < 2, other, own)
-        rows = pl.ds(pl.multiple_of(z * rows_q, rows_q), rows_q)
-        block = r1.at[:, rows, :]
-        drain(block, r1_sem.at[z])
+        place = lax.rem(me + n - step, half)
+        p = jnp.where(step < half, side, 1 - side) * half + place
+        rows = pl.ds(pl.multiple_of(p * sources, sources), sources)
+        drain(r1.at[:, rows, :], r1_sem.at[p])
         both = jnp.concatenate([r1[0, rows, :], r1[1, rows, :]], axis=0)
         prod = jnp.dot(both, gw[...], preferred_element_type=jnp.float32)
-        re = prod[:rows_q, :receivers] - prod[rows_q:, receivers:]
-        im = prod[:rows_q, receivers:] + prod[rows_q:, :receivers]
+        re = prod[:sources, :receivers] - prod[sources:, receivers:]
+        im = prod[:sources, receivers:] + prod[sources:, :receivers]
         mbuf[0, rows, :] = (re * scale_m).astype(jnp.bfloat16)
         mbuf[1, rows, :] = (im * scale_m).astype(jnp.bfloat16)
-
-        @pl.loop(0, quarter)
-        def _(q):
-            p = z * quarter + lax.rem(me + q, quarter)
-            src = mbuf.at[:, pl.ds(pl.multiple_of(p * sources, sources), sources), :]
-
-            @pl.when(p != me)
-            def _():
-                pltpu.make_async_remote_copy(
-                    src_ref=src, dst_ref=out_ref.at[me],
-                    send_sem=send_sem.at[3], recv_sem=out_sem,
-                    device_id={"freq": p}, device_id_type=pl.DeviceIdType.MESH,
-                ).start()
-
-            @pl.when(p == me)
-            def _():
-                pltpu.make_async_copy(src, out_ref.at[me], out_sem).start()
+        src = mbuf.at[:, rows, :]
+
+        @pl.when(p != me)
+        def _():
+            pltpu.make_async_remote_copy(
+                src_ref=src, dst_ref=out_ref.at[me],
+                send_sem=send_sem.at[3], recv_sem=out_sem,
+                device_id={"freq": p}, device_id_type=pl.DeviceIdType.MESH,
+            ).start()
+
+        @pl.when(p == me)
+        def _():
+            pltpu.make_async_copy(src, out_ref.at[me], out_sem).start()
 
     drain(out_ref, out_sem)
     for k in range(3):
@@ -191,17 +186,48 @@
             device_id={"freq": p}, device_id_type=pl.DeviceIdType.MESH,
         ).start()
 
-    @pl.loop(0, half)
-    def _(q):
-        send(peer_far(q))
-
-    @pl.loop(1, half)
-    def _(q):
-        send(peer_near(q))
-
-    pltpu.make_async_copy(
-        stage.at[k, me, :, here, :], landing.at[:, there, :], arrive
-    ).start()
+    def far():
+        @pl.loop(0, half)
+        def _(q):
+            send(peer_far(q))
+
+    def near():
+        pltpu.make_async_copy(
+            stage.at[k, me, :, here, :], landing.at[:, there, :], arrive
+        ).start()
+
+        @pl.loop(1, half)
+        def _(q):
+            send(peer_near(q))
+
+    if k == 2:
+        near()
+        far()
+    else:
+        far()
+        near()
+
+
+def inverse_kernel(piece_ref, table_ref, out_ref, scr):
+    count = piece_ref.shape[0]
+    step = pl.program_id(0)
+    sub = out_ref.shape[0]
+    per = GROUP // sub
+
+    @pl.when(lax.rem(step, per) == 0)
+    def _():
+        at = pl.ds(pl.multiple_of(step // per * GROUP, GROUP), GROUP)
+        for w in range(2 * count):
+            scr[:, w, :] = piece_ref[w // 2, w % 2, at, :].astype(jnp.float32)
+
+    scale = 1.0 / (count ** 0.5)
+    for s in range(sub):
+        row = lax.rem(step, per) * sub + s
+        timed = lax.dot_general(
+            scr[row].astype(jnp.bfloat16), table_ref[...],
+            (((0,), (0,)), ((), ())), preferred_element_type=jnp.float32,
+        )
+        out_ref[s] = (timed * scale).astype(jnp.bfloat16)
 
 
 def spectrum(traces, start, finish, table, count):
@@ -265,7 +291,7 @@
 def on_device(primary_one, primary_two, primary_three, window_start, window_end):
     sources, receivers, samples = primary_one.shape
     n = lax.axis_size("freq")
-    if sources % GROUP or n % 4 or receivers % 256 or samples % LANES:
+    if sources % GROUP or n % 2 or receivers % 256 or samples % LANES:
         return plain_on_device(
             primary_one, primary_two, primary_three, window_start, window_end
         )
@@ -292,7 +318,7 @@
             pltpu.VMEM((2, whole, receivers), bf),
             pltpu.SemaphoreType.DMA((2,)),
             pltpu.SemaphoreType.DMA((4,)),
-            pltpu.SemaphoreType.DMA((4,)),
+            pltpu.SemaphoreType.DMA((n,)),
             pltpu.SemaphoreType.DMA((2,)),
             pltpu.SemaphoreType.DMA,
         ],
@@ -301,12 +327,15 @@
         ),
         name="exchange",
     )(primary_one, primary_two, primary_three, window_start, window_end, table)
-    flat = piece.reshape(2 * count, sources * receivers)
-    timed = lax.dot_general(
-        flat, table, (((0,), (0,)), ((), ())), preferred_element_type=jnp.float32
-    )
-    timed = timed * (1.0 / jnp.sqrt(jnp.float32(count)))
-    return timed.astype(jnp.bfloat16).reshape(sources, receivers, samples)
+    return pl.pallas_call(
+        inverse_kernel,
+        out_shape=jax.ShapeDtypeStruct(primary_one.shape, bf),
+        grid=(sources // sub,),
+        in_specs=[vmem, vmem],
+        out_specs=pl.BlockSpec((sub, receivers, samples), lambda i: (i, 0, 0)),
+        scratch_shapes=[pltpu.VMEM((GROUP, 2 * count, receivers), jnp.float32)],
+        name="inverse",
+    )(piece, table)
 
 
 def solution(mesh):

time: 125 us -> 117 us (0.936)
  matrix products: 8.56 us -> 0 us
  Pallas kernels: 113 us -> 115 us
  local copies, waits for them, and re-layouts: 2.48 us -> 0.67 us
    pallas_call x0 -> x1, Pallas kernels: none -> 10.8 us  [on_device(): pl.pallas_call(inverse_kernel, out_shape=jax.ShapeDtypeStruct(primary_one...]
    dot_general x1 -> x0, matrix products: 8.56 us -> none  [on_device(): lax.dot_general(flat, table, (((0,), (0,)), ((), ())), preferred_element_...]
    pallas_call x1, Pallas kernels: 113 us -> 105 us  [on_device(): pl.pallas_call(functools.partial(exchange_kernel, n, sub), out_shape=jax....]
    unnamed x3 -> x0, local copies, waits for them, and re-layouts: 1.81 us -> none
where the time goes in v2:
time: 117 us; the launch traced here: 116 us
  Pallas kernels  115 us (98%)
    pallas_call x1, Pallas kernels, on_device(): pl.pallas_call(functools.partial(exchange_kernel, n, sub), out_shape=jax....  105 us
    pallas_call x1, Pallas kernels, on_device(): pl.pallas_call(inverse_kernel, out_shape=jax.ShapeDtypeStruct(primary_one...  10.8 us

profile of v2, /device:TPU:1, one launch (start us, length us, event | category | flops | bytes accessed | tf_op | source)
XLA Modules:
  0.0 116.2 jit_solution(4624027678285258838)
XLA Ops:
  0.0 0.2 cosine_convert_fusion
  0.3 0.6 convert_element_type.20.table_ref
  0.9 104.5 %exchange.1.piece_ref = bf16[16,2,32,512]{3,2,1,0:T(8,128)(2,1)} custom-call(bf16[32,512,512]{2,1,0:T(8,128)(2,1)} %one_ref.1, bf16[32,512,512]{2,1,0:T(8,128)(2,1)} %two_ref.1, bf16[32,512,512]{2,1,0:T(8,128)(2,1)} %three_ref.1, s32[3,32,512]{2,1,0:T(8,128)} %start_ref.1, s32[3,32,512]{2,1,0:T(8,128)} %end_ref.1, bf16[32,512]{1,0:T(8,128)(2,1)} %convert_element_type.20.table_ref), custom_call_target="tpu_custom_call" | custom-call | tf_op jit(solution)/shard_map/exchange/pallas_call | solution.py:305
  105.4 10.8 %inverse.1 = bf16[32,512,512]{2,1,0:T(8,128)(2,1)} custom-call(bf16[16,2,32,512]{3,2,1,0:T(8,128)(2,1)} %exchange.1.piece_ref, bf16[32,512]{1,0:T(8,128)(2,1)} %convert_element_type.20.table_ref), custom_call_target="tpu_custom_call" | custom-call | tf_op jit(solution)/shard_map/inverse/pallas_call | solution.py:330
  (3 shorter events, 0.0 us)
